TPU v7x, 32 devices: a whole 2x2x4 slice. The times are simulated.
32 devices in a mesh: docs: 2 (over x), seq: 16 (over z, y, core).
Axes of the slice: x: 2, y: 2, z: 4, core: 2. Of those that a mesh axis runs over, the one named last changes fastest.
Arguments:
- hidden_in: bfloat16 [8192, 4096], P(('docs', 'seq')), parts along dimension 0, may hold values from -6 to 6
- mix_norm_gain: float32 [4096], replicated, may hold values from 0.5 to 1.5
- ssm_proj: bfloat16 [4096, 64], replicated, may hold values from -0.09375 to 0.09375
- dt_bias: float32 [32], replicated, may hold values from -1 to 1
- decay_rate: float32 [32], replicated, may hold values from 4.8828124e-06 to 0.05
- mixer_gain: float32 [4096], replicated, may hold values from 0.5 to 1.5
- ffn_norm_gain: float32 [4096], replicated, may hold values from 0.5 to 1.5
- router: bfloat16 [4096, 16], replicated, may hold values from -0.09375 to 0.09375
- routes: int32 [8192, 2], P(('docs', 'seq')), parts along dimension 0, may hold values from 0 to 15, as said below
- w_gate: bfloat16 [4096, 3584], P(None, 'seq'), may hold values from -0.09375 to 0.09375
- w_up: bfloat16 [4096, 3584], P(None, 'seq'), may hold values from -0.09375 to 0.09375
- w_down: bfloat16 [3584, 4096], P('seq'), may hold values from -0.09375 to 0.09375
Outputs:
- block_out: bfloat16 [8192, 4096], P(('docs', 'seq')), parts along dimension 0
There are 2 independent parts, one for each index of `docs`. A program takes and returns all parts, laid end to end along the dimension named above; an argument that names none is the same for every part. Nothing has to cross between parts.
Inputs may be any that keep to these rules, and one draw needn't show every extreme that they name: `routes`: each token names two different experts. Among the 256 tokens of one device at most 16 name expert 0, and on some device exactly 16 do.
All inputs are finite; a program needn't handle non-finite values.
Results may differ from a plain program's by a relative error of at most 0.0056.
Values may be sent and summed in bfloat16 or wider, within the bound.
A program may use at most 128 MiB of HBM per device.

v0:
```python
import jax
import jax.numpy as jnp
from jax import lax
from jax.sharding import PartitionSpec as P

SPAN = 128
CAP = 16


EPSILON = 1e-05
HIGHEST_MODE = lax.Precision.HIGHEST


def entering_2(part, axis, combine, identity):
    place = lax.axis_index(axis)
    gathered = jax.tree.map(lambda a: lax.all_gather(a, axis), part)
    state = jax.tree.map(lambda a, e: jnp.zeros_like(a) + jnp.asarray(e, a.dtype), part, identity)

    def one(turn, state):
        return combine(
            state, jax.tree.map(lambda a: lax.dynamic_index_in_dim(a, turn, 0, False), gathered)
        )

    return lax.fori_loop(0, place, one, state)


def rms_scale(values, gain_row):
    return (
        values * lax.rsqrt(jnp.mean(values * values, axis=-1, keepdims=True) + EPSILON) * gain_row
    )


def span_output(span_x, span_b, span_c, span_dt, span_cum, entering):
    row_count = span_cum.shape[0]
    lower_mask = jnp.arange(row_count)[:, None] >= jnp.arange(row_count)[None, :]
    cross_dot = jnp.dot(span_c, span_b.T, precision=HIGHEST_MODE)
    log_gap = span_cum.T[:, :, None] - span_cum.T[:, None, :]
    decays = jnp.where(lower_mask[None], jnp.exp(jnp.minimum(log_gap, 0.0)), 0.0)
    weights = (cross_dot[None] * decays * span_dt.T[:, None, :]).astype(jnp.bfloat16)
    within = jnp.einsum("hts,shp->thp", weights, span_x, preferred_element_type=jnp.float32)
    carried = jnp.exp(span_cum)[:, :, None] * jnp.einsum(
        "tn,hpn->thp", span_c, entering, precision=HIGHEST_MODE
    )
    return within + carried


def span_state(span_x, span_b, span_dt, span_cum):
    to_end = jnp.exp(span_cum[-1][None, :] - span_cum) * span_dt
    state_weights = (to_end[:, :, None] * span_b[:, None, :]).astype(jnp.bfloat16)
    return jnp.einsum("shp,shn->hpn", span_x, state_weights, preferred_element_type=jnp.float32)


def link_states(earlier, later_pair):
    return (earlier[0] * later_pair[0], later_pair[0][:, None, None] * earlier[1] + later_pair[1])


def chain_entry(overall, end_state):
    identity = (jnp.ones_like(overall), jnp.zeros_like(end_state))
    before = entering_2((overall, end_state), "seq", link_states, identity)
    return before[1]


def route_gates(logits, routes):
    expert_ids = jnp.arange(logits.shape[1], dtype=jnp.int32)
    chosen_logit = jnp.sum(
        jnp.where(routes[:, :, None] == expert_ids[None, None, :], logits[:, None, :], 0.0), axis=2
    )
    first_zero = routes[:, 0] == 0
    routed = first_zero | (routes[:, 1] == 0)
    second_logit = jnp.where(first_zero, chosen_logit[:, 1], chosen_logit[:, 0])
    gating = jnp.where(routed, jax.nn.sigmoid(logits[:, 0] - second_logit), 0.0)
    return (gating, routed)


def body(
    hidden_in,
    mix_norm_gain,
    ssm_proj,
    dt_bias,
    decay_rate,
    mixer_gain,
    ffn_norm_gain,
    router,
    routes,
    w_gate,
    w_up,
    w_down,
):
    tok_rows, model_width = hidden_in.shape
    head_count = dt_bias.shape[0]
    state_size = (ssm_proj.shape[1] - head_count) // 2
    head_size = model_width // head_count
    wide_input = hidden_in.astype(jnp.float32)
    normed = rms_scale(wide_input, mix_norm_gain).astype(jnp.bfloat16)
    projected = jnp.dot(normed, ssm_proj, preferred_element_type=jnp.float32)
    b_in = projected[:, :state_size]
    c_out = projected[:, state_size : 2 * state_size]
    step_size = jax.nn.softplus(projected[:, 2 * state_size :] + dt_bias)
    log_decay = -step_size * decay_rate
    heads_x = normed.reshape(tok_rows, head_count, head_size)
    lower_ones = (jnp.arange(SPAN)[:, None] >= jnp.arange(SPAN)[None, :]).astype(jnp.float32)
    entering = jnp.zeros((head_count, head_size, state_size), jnp.float32)
    offset = jnp.zeros((head_count,), jnp.float32)
    offsets = []
    outputs = []
    for number in range(tok_rows // SPAN):
        opening = number * SPAN
        closing = opening + SPAN
        span_cum = jnp.dot(lower_ones, log_decay[opening:closing], precision=HIGHEST_MODE)
        span_x = heads_x[opening:closing]
        span_b = b_in[opening:closing]
        span_dt = step_size[opening:closing]
        outputs.append(
            span_output(span_x, span_b, c_out[opening:closing], span_dt, span_cum, entering)
        )
        offsets.append(span_cum + offset)
        entering = jnp.exp(span_cum[-1])[:, None, None] * entering + span_state(
            span_x, span_b, span_dt, span_cum
        )
        offset = offset + span_cum[-1]
    chain_in = chain_entry(jnp.exp(offset), entering)
    device_cum = jnp.concatenate(offsets, axis=0)
    ssm_out = jnp.concatenate(outputs, axis=0) + jnp.exp(device_cum)[:, :, None] * jnp.einsum(
        "tn,hpn->thp", c_out, chain_in, precision=HIGHEST_MODE
    )
    scaled = (
        ssm_out
        * lax.rsqrt(jnp.mean(ssm_out * ssm_out, axis=-1, keepdims=True) + EPSILON)
        * mixer_gain.reshape(head_count, head_size)
    )
    after_mixer = (wide_input + scaled.reshape(tok_rows, model_width)).astype(jnp.bfloat16)
    ffn_in = rms_scale(after_mixer.astype(jnp.float32), ffn_norm_gain).astype(jnp.bfloat16)
    logits = jnp.dot(ffn_in, router, preferred_element_type=jnp.float32)
    gating, routed = route_gates(logits, routes)
    slot_rank = jnp.cumsum(routed.astype(jnp.int32)) - 1
    slot_ids = jnp.arange(CAP, dtype=jnp.int32)
    select_map = routed[None, :] & (slot_rank[None, :] == slot_ids[:, None])
    slot_rows = jnp.dot(
        select_map.astype(jnp.bfloat16), ffn_in, preferred_element_type=jnp.float32
    ).astype(jnp.bfloat16)
    gathered = lax.all_gather(slot_rows, "seq", axis=0, tiled=True)
    gate_part = jnp.dot(gathered, w_gate, preferred_element_type=jnp.float32)
    up_part = jnp.dot(gathered, w_up, preferred_element_type=jnp.float32)
    hidden = (jax.nn.silu(gate_part) * up_part).astype(jnp.bfloat16)
    partial_value = jnp.dot(hidden, w_down, preferred_element_type=jnp.float32)
    received = lax.all_to_all(
        partial_value.astype(jnp.bfloat16), "seq", split_axis=0, concat_axis=0, tiled=True
    ).astype(partial_value.dtype)
    own_rows = jnp.sum(received.reshape(-1, CAP, model_width), axis=0)
    returned = jnp.dot(select_map.astype(jnp.float32).T, own_rows, precision=HIGHEST_MODE)
    return (after_mixer.astype(jnp.float32) + gating[:, None] * returned).astype(jnp.bfloat16)


def solution(mesh):
    in_specs = (
        P(("docs", "seq"), None),
        P(),
        P(),
        P(),
        P(),
        P(),
        P(),
        P(),
        P(("docs", "seq"), None),
        P(None, "seq"),
        P(None, "seq"),
        P("seq", None),
    )
    out_specs = P(("docs", "seq"), None)
    return jax.shard_map(body, mesh=mesh, in_specs=in_specs, out_specs=out_specs, check_vma=False)
```

profile of v0, /device:TPU:0, one launch (start us, length us, event | category | flops | bytes accessed | tf_op | source)
XLA Modules:
  0.0 232.9 jit_solution(10469629483626832132)
XLA Ops:
  6.5 2.2 fusion.1
  8.9 1.3 fusion.3
  10.3 1.5 fusion.64
  11.7 0.8 fusion.67
  13.0 1.7 copy.40
  15.0 2.3 copy.38
  17.3 1.9 convolution_add_fusion.1
  19.1 1.4 convolution_add_fusion
  20.6 23.2 %all-gather.1 = f32[16,1,32]{2,1,0:T(1,128)S(1)} all-gather(f32[1,1,32]{2,1,0:T(1,128)S(1)} %bitcast.69), channel_id=1, replica_groups=mesh['docs'=2,'seq'=16] {'seq'}, dimensions={0}, use_global_device_ids=true | all-gather | bytes 2176 | tf_op jit(solution)/shard_map/all_gather | solution.py:16
  43.8 0.3 fusion.51
  44.1 0.3 fusion.54
  44.4 1.0 fusion.33
  45.4 1.8 fusion.43
  47.3 2.3 bitcast_add_fusion.1
  49.5 2.3 bitcast_add_fusion.2
  51.8 22.1 %all-gather.7.cloned.1.call-done = f32[512,128,16]{1,2,0:T(8,128)} async-done(((f32[32,128,16]{1,2,0:T(8,128)}), f32[512,128,16]{1,2,0:T(8,128)}) %all-gather.7.cloned.1.call-update) | async-done | bytes 4194320 | tf_op jit(solution)/shard_map/all_gather | solution.py:16
  74.2 6.6 %multiply_reduce_fusion = (f32[256,32]{0,1:T(8,128)S(1)}, f32[256,32,128]{2,0,1:T(8,128)S(1)}) fusion(f32[32,128,16]{1,2,0:T(8,128)S(1)} %get-tuple-element.49, f32[256,64]{0,1:T(8,128)S(1)} %fusion.67, f32[256,32]{0,1:T(8,128)S(1)} %maximum_exponential_fusion, f32[128,32,128]{2,0,1:T(8,128)} %bitcast_add_fusion.1, f32[128,32,128]{2,0,1:T(8,128)} %bitcast_add_fusion.2), kind=kOutput, calls=%fused_computation.22 | convolution fusion | flops 206561280 | bytes 8732672 | tf_op jit(solution)/shard_map/tn,hpn->thp/dot_general | solution.py:123
  80.8 3.1 %multiply_multiply_fusion = f32[256,32,128]{2,0,1:T(8,128)} fusion(f32[256,32,128]{2,0,1:T(8,128)S(1)} %get-tuple-element.83, f32[32,128]{1,0:T(8,128)S(1)} %bitcast.65, f32[256,32]{0,1:T(8,128)S(1)} %add_rsqrt_fusion), kind=kLoop, calls=%fused_computation.21 | loop fusion | flops 2097152 | bytes 8437760 | tf_op jit(solution)/shard_map/mul | solution.py:127
  83.9 5.6 %copy.45 = f32[256,32,128]{0,2,1:T(8,128)} copy(f32[256,32,128]{2,0,1:T(8,128)} %multiply_multiply_fusion) | data formatting | bytes 8388608 | tf_op jit(solution)/shard_map/mul | solution.py:127
  89.5 5.6 %copy.46 = f32[256,4096]{1,0:T(8,128)} copy(f32[256,4096]{0,1:T(8,128)} %bitcast.56) | data formatting | bytes 8388608 | tf_op jit(solution)/shard_map/reshape | solution.py:131
  95.2 3.7 %fusion.5 = (f32[256]{0:T(256)S(1)}, bf16[256,4096]{1,0:T(8,128)(2,1)S(1)}) fusion(f32[256,4096]{1,0:T(8,128)} %copy.46, bf16[256,4096]{1,0:T(8,128)(2,1)} %param.14), kind=kLoop, calls=%fused_computation.16 | loop fusion | flops 6291200 | bytes 8389632 | tf_op jit(solution)/shard_map/reduce_sum | solution.py:29
  98.9 1.3 copy-done.2
  100.2 0.7 fusion.22
  101.0 0.3 reduce-window.9
  101.6 2.9 %convolution_convert_fusion.1 = bf16[16,4096]{1,0:T(8,128)(2,1)} fusion(bf16[256,4096]{1,0:T(8,128)(2,1)} %copy-done.2, f32[4096]{0:T(1024)S(1)} %copy-done.11, f32[256]{0:T(256)S(1)} %add_rsqrt_fusion.1, s32[256]{0:T(256)S(1)} %add_bitcast_fusion, pred[256]{0:T(512)(128)(4,1)S(1)} %get-tuple-element.80), kind=kOutput, calls=%fused_computation.11 | convolution fusion | flops 37822464 | bytes 2246912 | tf_op jit(solution)/shard_map/dot_general | solution.py:138
  104.6 56.7 %all-gather.5.cloned.1.call-done = bf16[256,4096]{1,0:T(8,128)(2,1)} async-done(((bf16[16,4096]{1,0:T(8,128)(2,1)}), bf16[256,4096]{1,0:T(8,128)(2,1)}) %all-gather.5.cloned.1.call-update) | async-done | bytes 2097168 | tf_op jit(solution)/shard_map/all_gather | solution.py:141
  161.3 2.9 %fusion.68 = f32[256,224]{0,1:T(8,128)S(1)} fusion(bf16[256,4096]{1,0:T(8,128)(2,1)} %all-gather.5.cloned.1.call-done, bf16[4096,224]{0,1:T(8,128)(2,1)} %param.23), kind=kOutput, calls=%fused_computation.113 | convolution fusion | flops 469762048 | bytes 4161536 | tf_op jit(solution)/shard_map/dot_general | solution.py:142
  164.2 5.9 %convolution_convert_fusion = bf16[256,4096]{1,0:T(8,128)(2,1)} fusion(bf16[224,4096]{1,0:T(8,128)(2,1)S(1)} %copy-done, bf16[256,4096]{1,0:T(8,128)(2,1)} %all-gather.5.cloned.1.call-done, bf16[4096,224]{0,1:T(8,128)(2,1)} %param.24, f32[256,224]{0,1:T(8,128)S(1)} %fusion.68), kind=kOutput, calls=%fused_computation.10 | convolution fusion | flops 940916736 | bytes 8093696 | tf_op jit(solution)/shard_map/dot_general | solution.py:145
  170.1 50.8 %all_to_all.9 = bf16[16,16,4096]{2,1,0:T(8,128)(2,1)S(1)} all-to-all(bf16[16,16,4096]{2,1,0:T(8,128)(2,1)} %bitcast.57), channel_id=1, replica_groups=mesh['docs'=2,'seq'=16] {'seq'}, dimensions={0} | all-to-all | bytes 4194304 | tf_op jit(solution)/shard_map/all_to_all | solution.py:146
  221.0 0.3 convert_reduce_fusion
  221.3 1.3 copy-done.3
  222.5 3.5 %fusion = bf16[256,4096]{1,0:T(8,128)(2,1)} fusion(f32[16,4096]{1,0:T(8,128)S(1)} %convert_reduce_fusion, bf16[256,4096]{1,0:T(8,128)(2,1)S(1)} %copy-done.3, f32[256]{0:T(256)S(1)} %bitcast.67, s32[256]{0:T(256)S(1)} %add_bitcast_fusion, pred[256]{0:T(512)(128)(4,1)S(1)} %get-tuple-element.80), kind=kOutput, calls=%fused_computation.9 | convolution fusion | flops 205529088 | bytes 4458752 | tf_op jit(solution)/shard_map/dot_general | solution.py:150
  (48 shorter events, 1.6 us)
Async XLA Ops:
  6.5 157.7 %copy-start = (bf16[224,4096]{1,0:T(8,128)(2,1)S(1)}, bf16[224,4096]{1,0:T(8,128)(2,1)}, u32[]{:S(2)}) copy-start(bf16[224,4096]{1,0:T(8,128)(2,1)} %param.25) | copy-start | bytes 5505028
  6.5 67.4 %all-gather.7.cloned.1.call-start = ((), (), s32[]{:S(2)}) async-start(), calls=%async_computation.2 | async-start | bytes 4456448 | tf_op jit(solution)/shard_map/all_gather | solution.py:16
  6.5 2.4 %copy-start.1 = (bf16[256,4096]{1,0:T(8,128)(2,1)S(1)}, bf16[256,4096]{1,0:T(8,128)(2,1)}, u32[]{:S(2)}) copy-start(bf16[256,4096]{1,0:T(8,128)(2,1)} %param.14) | copy-start | bytes 6291460
  10.3 1.5 copy-start.5
  11.7 0.8 copy-start.8
  11.7 0.8 copy-start.9
  20.5 140.7 %all-gather.5.cloned.1.call-start = ((), (), s32[]{:S(2)}) async-start(), calls=%async_computation.1 | async-start | bytes 2228224 | tf_op jit(solution)/shard_map/all_gather | solution.py:141
  47.2 2.3 copy-start.4
  74.2 6.6 %copy-start.6 = (f32[4096]{0:T(1024)S(1)}, f32[4096]{0:T(1024)}, u32[]{:S(2)}) copy-start(f32[4096]{0:T(1024)} %param.19) | copy-start | bytes 49156
  95.2 5.1 %copy-start.10 = (bf16[4096,16]{0,1:T(8,128)(2,1)S(1)}, bf16[4096,16]{0,1:T(8,128)(2,1)}, u32[]{:S(2)}) copy-start(bf16[4096,16]{0,1:T(8,128)(2,1)} %param.21) | copy-start | bytes 393220
  95.2 5.1 %copy-start.11 = (f32[4096]{0:T(1024)S(1)}, f32[4096]{0:T(1024)}, u32[]{:S(2)}) copy-start(f32[4096]{0:T(1024)} %param.20) | copy-start | bytes 49156
  98.9 1.3 copy-start.2
  98.9 2.0 copy-start.7
  221.0 1.6 copy-start.3
Sparse Core Ops, SparseCore 0:
  20.7 53.2 all-gather.6
  104.7 56.5 all-gather.4
where the time goes:
time: 234 us; the launch traced here: 233 us
  waiting for transfers between devices  78.9 us (34%)
  blocking collectives  74 us (32%)
  matrix products  34.9 us (15%)
  local copies, waits for them, and re-layouts  19.6 us (8%)
  between operations  13.6 us (6%)
  other arithmetic  11.6 us (5%)
    all_gather x1, waiting for transfers between devices, body(): gathered = lax.all_gather(slot_rows, 'seq', axis=0, tiled=True)  56.7 us
    all_to_all x1, blocking collectives, body(): lax.all_to_all(partial_value.astype(jnp.bfloat16), 'seq', split_axis=0, c...  50.8 us
    all_gather x1, blocking collectives, entering_2(): gathered = jax.tree.map(lambda a: lax.all_gather(a, axis), part)  23.2 us
    all_gather x1, waiting for transfers between devices, entering_2(): gathered = jax.tree.map(lambda a: lax.all_gather(a, axis), part)  22.1 us
    dot_general x1, matrix products, body(): jnp.einsum('tn,hpn->thp', c_out, chain_in, precision=HIGHEST_MODE)  6.56 us
    reduce_sum x2, other arithmetic, rms_scale(): jnp.mean(values * values, axis=-1, keepdims=True) + EPSILON  5.96 us
    dot_general x1, matrix products, body(): partial_value = jnp.dot(hidden, w_down, preferred_element_type=jnp.float32)  5.93 us
    reshape x1, local copies, waits for them, and re-layouts, body(): scaled.reshape(tok_rows, model_width)  5.65 us
  transfers between devices with their start and end apart: 2, of which 2 were waited for; matrix products, arithmetic and copies ran while one was open for 3% of the time, Pallas kernels for 0%

commit v1 on v0

v1 whole, which is shorter than its diff:
```python
import functools

import jax
import jax.numpy as jnp
from jax import lax
from jax.experimental import pallas as pl
from jax.experimental.pallas import tpu as pltpu
from jax.sharding import PartitionSpec as P

CAP = 16
EPS = 1e-05
HI = lax.Precision.HIGHEST
MESH = pl.DeviceIdType.MESH
F32 = jnp.float32
BF16 = jnp.bfloat16


def remote(src, dst, send, recv, target):
    return pltpu.make_async_remote_copy(
        src_ref=src,
        dst_ref=dst,
        send_sem=send,
        recv_sem=recv,
        device_id={"seq": target},
        device_id_type=MESH,
    )


def iota(shape, dim):
    return lax.broadcasted_iota(jnp.int32, shape, dim)


def block_kernel(
    n,
    hid,
    gain,
    proj,
    bias,
    rate,
    mgain,
    fgain,
    router,
    routes,
    wg_hbm,
    wu_hbm,
    wd_hbm,
    am_out,
    own_out,
    sel_out,
    gate_out,
    wg,
    wu,
    wd,
    xn,
    within,
    am,
    acc,
    cum3,
    cumt,
    dtt,
    tet,
    bt,
    crossm,
    phi,
    plo,
    msg,
    inbox,
    scan_out,
    ent,
    gath,
    part,
    prt,
    rbuf,
    w_sem,
    am_sem,
    a_send,
    a_recv,
    b_send,
    b_recv,
    g_send,
    g_recv,
    d_send,
    d_recv,
    p_send,
    p_recv,
    r_send,
    r_recv,
):
    tok, width = hid.shape
    heads = bias.shape[0]
    lanes = width // heads
    state = (proj.shape[1] - heads) // 2
    owners = msg.shape[0]
    per = heads // owners
    chips = n // 2
    half_ring = chips // 2
    hw = width // 2
    me = lax.axis_index("seq")
    core = me % 2
    chip = me // 2
    odd = chip % 2
    pos = (1 - odd) * (chip // 2) + odd * (chips - 1 - chip // 2)

    def device_at(place):
        place = (place + 2 * chips) % chips
        high = place // half_ring
        held = (1 - high) * (2 * place) + high * (2 * (chips - 1 - place) + 1)
        return held * 2 + core

    def slot_at(place, which):
        return which * chips + (place + 2 * chips) % chips

    partner = me + 1 - 2 * core

    barrier = pltpu.get_barrier_semaphore()
    for d in range(1, n):
        pl.semaphore_signal(
            barrier, inc=1, device_id={"seq": (me + d) % n}, device_id_type=MESH
        )

    loads = [
        pltpu.make_async_copy(a, b, w_sem.at[k])
        for k, (a, b) in enumerate(((wg_hbm, wg), (wu_hbm, wu), (wd_hbm, wd)))
    ]
    for load in loads:
        load.start()

    def norm_rows(i, _):
        rows = pl.ds(pl.multiple_of(i * 16, 16), 16)
        x = hid[rows, :].astype(F32)
        ms = jnp.mean(x * x, axis=-1, keepdims=True)
        xn[rows, :] = (x * lax.rsqrt(ms + EPS) * gain[...]).astype(BF16)
        return 0

    lax.fori_loop(0, tok // 16, norm_rows, 0)

    p = jnp.dot(xn[...], proj[...], preferred_element_type=F32)
    p_hi = p.astype(BF16)
    phi[...] = p_hi
    plo[...] = (p - p_hi.astype(F32)).astype(BF16)
    pt = p.T
    b_t = pt[0:state]
    v = pt[2 * state :] + bias[...]
    dt = jnp.maximum(v, 0.0) + jnp.log(1.0 + jnp.exp(-jnp.abs(v)))
    upper = (iota((tok, tok), 0) <= iota((tok, tok), 1)).astype(F32)
    c_t = jnp.dot(-dt * rate[...], upper, precision=HI, preferred_element_type=F32)
    bt[...] = b_t
    dtt[...] = dt
    cumt[...] = c_t
    tet[...] = jnp.exp(c_t[:, tok - 1 : tok] - c_t) * dt
    c1 = c_t.astype(BF16).astype(F32)
    c2 = (c_t - c1).astype(BF16).astype(F32)
    c3 = c_t - c1 - c2
    pad = jnp.zeros((128 - 3 * heads, tok), F32)
    cum3[...] = jnp.concatenate([c1, c2, c3, pad], axis=0).T.astype(BF16)

    def spread(h):
        row = iota((128, lanes), 0)
        pick = ((row % heads) == h) & (row < 3 * heads)
        return jnp.where(pick, 1.0, 0.0).astype(BF16)

    def state_head(h, _):
        cols = pl.ds(pl.multiple_of(h * lanes, lanes), lanes)
        inner = pl.ds(pl.multiple_of((h % per) * lanes, lanes), lanes)
        sw = (bt[...] * tet[pl.ds(h, 1), :]).astype(BF16)
        s = jnp.dot(sw, xn[:, cols], preferred_element_type=F32)
        msg[h // per, 0:state, inner] = s.astype(BF16)
        last = jnp.dot(cum3[tok - 16 : tok, :], spread(h), preferred_element_type=F32)
        d = jnp.exp(last[15:16, :])
        d_hi = d.astype(BF16).astype(F32)
        row = iota((16, lanes), 0)
        packed = jnp.where(row == 0, d_hi, jnp.where(row == 1, d - d_hi, 0.0))
        msg[h // per, state : state + 16, inner] = packed.astype(BF16)
        return 0

    lax.fori_loop(0, heads, state_head, 0)

    pl.semaphore_wait(barrier, n - 1)

    def to_owner(owner, source):
        return remote(
            msg.at[owner], inbox.at[source], a_send.at[owner], a_recv.at[source], owner
        )

    def to_reader(reader, source):
        return remote(
            scan_out.at[reader],
            ent.at[source],
            b_send.at[reader],
            b_recv.at[source],
            reader,
        )

    every = owners == n

    def for_owner(index, run):
        if every:
            run()
        else:
            pl.when(index < owners)(run)

    for d in range(1, n):
        dest = (me + d) % n
        for_owner(dest, lambda: to_owner(dest, me).start())

    z = jnp.concatenate(
        [
            jnp.zeros((state, tok), F32),
            bt[...],
            jnp.zeros((p.shape[1] - 2 * state, tok), F32),
        ],
        axis=0,
    )
    cross = jnp.dot(p, z, precision=HI, preferred_element_type=F32)
    crossm[...] = jnp.where(iota((tok, tok), 0) >= iota((tok, tok), 1), cross, 0.0)

    mid = tok // 2

    def within_head(h, _):
        cols = pl.ds(pl.multiple_of(h * lanes, lanes), lanes)
        ch = jnp.dot(cum3[...], spread(h), preferred_element_type=F32)
        crow = cumt[pl.ds(h, 1), :]
        drow = dtt[pl.ds(h, 1), :]
        for k in range(2):
            rows = slice(k * mid, (k + 1) * mid)
            total = None
            for j in range(k + 1):
                over = slice(j * mid, (j + 1) * mid)
                gap = ch[rows, :] - crow[:, over]
                w = crossm[rows, over] * jnp.exp(jnp.minimum(gap, 0.0)) * drow[:, over]
                term = jnp.dot(
                    w.astype(BF16), xn[over, cols], preferred_element_type=F32
                )
                total = term if total is None else total + term
            within[rows, cols] = total
        return 0

    lax.fori_loop(0, heads // 2, within_head, 0)

    def scan_all():
        inbox[me] = msg[me]
        for d in range(1, n):
            to_owner(0, (me + d) % n).wait_recv()
        running = jnp.zeros((state, per * lanes), F32)
        for j in range(n):
            scan_out[j] = running.astype(BF16)
            decay = (
                inbox[j, state : state + 1, :].astype(F32)
                + inbox[j, state + 1 : state + 2, :].astype(F32)
            )
            running = decay * running + inbox[j, 0:state, :].astype(F32)
        ent[me] = scan_out[me]
        for d in range(1, n):
            dest = (me + d) % n
            to_reader(dest, me).start()

    for_owner(me, scan_all)

    lax.fori_loop(heads // 2, heads, within_head, 0)

    for d in range(1, n):
        source = (me + d) % n
        for_owner(source, lambda: to_reader(0, source).wait_recv())

    acc[...] = jnp.zeros_like(acc)

    def mix_head(h, _):
        cols = pl.ds(pl.multiple_of(h * lanes, lanes), lanes)
        inner = pl.ds(pl.multiple_of((h % per) * lanes, lanes), lanes)
        e = ent[h // per, :, inner]
        zero = jnp.zeros((state, lanes), BF16)
        rest = jnp.zeros((phi.shape[1] - 2 * state, lanes), BF16)
        ez = jnp.concatenate([zero, e, rest], axis=0)
        carried = jnp.dot(phi[...], ez, preferred_element_type=F32) + jnp.dot(
            plo[...], ez, preferred_element_type=F32
        )
        ch = jnp.dot(cum3[...], spread(h), preferred_element_type=F32)
        o = within[:, cols] + jnp.exp(ch) * carried
        ms = jnp.mean(o * o, axis=-1, keepdims=True)
        y = hid[:, cols].astype(F32) + o * lax.rsqrt(ms + EPS) * mgain[:, cols]
        y = y.astype(BF16)
        am[:, cols] = y
        yf = y.astype(F32)
        acc[...] += yf * yf
        return 0

    lax.fori_loop(0, heads, mix_head, 0)

    am_copy = pltpu.make_async_copy(am, am_out, am_sem)
    am_copy.start()

    total = jnp.sum(acc[...], axis=-1, keepdims=True)
    acc[...] = jnp.broadcast_to(lax.rsqrt(total / width + EPS), acc.shape)

    def ffn_rows(i, _):
        rows = pl.ds(pl.multiple_of(i * 16, 16), 16)
        x = am[rows, :].astype(F32)
        xn[rows, :] = (x * acc[rows, 0:1] * fgain[...]).astype(BF16)
        return 0

    lax.fori_loop(0, tok // 16, ffn_rows, 0)

    r0 = routes[:, 0:1]
    r1 = routes[:, 1:2]
    hit = jnp.where((r0 == 0) | (r1 == 0), 1.0, 0.0)
    lower = (iota((tok, tok), 0) >= iota((tok, tok), 1)).astype(BF16)
    wide = jnp.broadcast_to(hit, (tok, 128))
    rank = jnp.dot(lower, wide.astype(BF16), preferred_element_type=F32)
    lane = iota((tok, 128), 1)
    place = (rank - 1.0).astype(jnp.int32)
    sel_t = jnp.where(((lane % CAP) == place) & (lane < 2 * CAP), wide, 0.0)
    sel = sel_t.T[0:CAP].astype(BF16)
    sel_out[...] = sel_t.astype(BF16)
    mine = slot_at(pos, core)
    gath[mine] = jnp.dot(sel, xn[...], preferred_element_type=F32).astype(BF16)

    def cut(h):
        return pl.ds(h * hw, hw)

    def ring(way, s, h, place):
        step = 1 - 2 * way
        block = gath.at[slot_at(place, core), :, cut(h)]
        return remote(
            block,
            block,
            g_send.at[way, s, h],
            g_recv.at[way, s, h],
            device_at(pos + step),
        )

    def across(way, s, h, place, which):
        block = gath.at[slot_at(place, which), :, cut(h)]
        return remote(
            block, block, d_send.at[way, s, h], d_recv.at[way, s, h], partner
        )

    started = []

    def go(copy):
        copy.start()
        started.append(copy)

    def used(way, s, h):
        return s < half_ring - 1 or h == way

    for h in range(2):
        for way in range(2):
            hh = h if way == 0 else 1 - h
            if used(way, 0, hh):
                go(ring(way, 0, hh, pos))
    def own_across(h, slot):
        block = gath.at[slot, :, cut(h)]
        return remote(
            block,
            block,
            d_send.at[h, half_ring, 0],
            d_recv.at[h, half_ring, 0],
            partner,
        )

    for h in range(2):
        go(own_across(h, mine))

    logits = jnp.dot(xn[...], router[...], preferred_element_type=F32)
    other = jnp.where(r0 == 0, r1, r0)
    picked = jnp.sum(
        jnp.where(iota(logits.shape, 1) == other, logits, 0.0), axis=1, keepdims=True
    )
    gate = jnp.where(hit > 0.0, 1.0 / (1.0 + jnp.exp(picked - logits[:, 0:1])), 0.0)
    gate_out[...] = jnp.broadcast_to(gate, gate_out.shape)

    for s in range(half_ring):
        for h in range(2):
            for way in range(2):
                hh = h if way == 0 else 1 - h
                if not used(way, s, hh):
                    continue
                step = 1 - 2 * way
                place = pos - step * (1 + s)
                ring(way, s, hh, place).wait_recv()
                if s + 1 < half_ring and used(way, s + 1, hh):
                    go(ring(way, s + 1, hh, place))
                go(across(way, s, hh, place, core))
    for h in range(2):
        own_across(h, slot_at(pos, 1 - core)).wait_recv()
    for s in range(half_ring):
        for way in range(2):
            for h in range(2):
                if used(way, s, h):
                    step = 1 - 2 * way
                    across(way, s, h, pos - step * (1 + s), 1 - core).wait_recv()

    for load in loads:
        load.wait()
    rows_all = n * CAP
    x_all = gath[...].reshape(rows_all, width)
    g = jnp.dot(x_all, wg[...], preferred_element_type=F32)
    u = jnp.dot(x_all, wu[...], preferred_element_type=F32)
    hidden = (g / (1.0 + jnp.exp(-g)) * u).astype(BF16)
    step_w = 512
    for k in range(width // step_w):
        c = slice(k * step_w, (k + 1) * step_w)
        part[:, :, c] = (
            jnp.dot(hidden, wd[:, c], preferred_element_type=F32)
            .astype(BF16)
            .reshape(n, CAP, step_w)
        )
    swap = remote(
        part.at[pl.ds((1 - core) * chips, chips)], prt, p_send, p_recv, partner
    )
    go(swap)
    swap.wait_recv()

    def pair_sum(i, _):
        at = core * chips + i
        part[at] = (part[at].astype(F32) + prt[i].astype(F32)).astype(BF16)
        return 0

    lax.fori_loop(0, chips, pair_sum, 0)

    def reduce_copy(way, s, h):
        step = 1 - 2 * way
        place = pos + step * (half_ring - s)
        return remote(
            part.at[slot_at(place, core), :, cut(h)],
            rbuf.at[way, s, h],
            r_send.at[way, s, h],
            r_recv.at[way, s, h],
            device_at(pos + step),
        )

    def carries(way, s, h):
        return s > 0 or h == way

    for s in range(half_ring):
        for h in range(2):
            for way in range(2):
                hh = h if way == 0 else 1 - h
                if not carries(way, s, hh):
                    continue
                if s > 0 and carries(way, s - 1, hh):
                    reduce_copy(way, s - 1, hh).wait_recv()
                    step = 1 - 2 * way
                    at = slot_at(pos + step * (half_ring - s), core)
                    cc = slice(hh * hw, (hh + 1) * hw)
                    part[at, :, cc] = (
                        part[at, :, cc].astype(F32)
                        + rbuf[way, s - 1, hh].astype(F32)
                    ).astype(BF16)
                go(reduce_copy(way, s, hh))
    for h in range(2):
        cc = slice(h * hw, (h + 1) * hw)
        own = part[mine, :, cc].astype(F32)
        for way in range(2):
            if carries(way, half_ring - 1, h):
                reduce_copy(way, half_ring - 1, h).wait_recv()
                own += rbuf[way, half_ring - 1, h].astype(F32)
        own_hi = own.astype(BF16)
        own_out[0:CAP, cc] = own_hi
        own_out[CAP : 2 * CAP, cc] = (own - own_hi.astype(F32)).astype(BF16)

    am_copy.wait()
    for copy in started:
        copy.wait_send()
    for d in range(1, n):
        dest = (me + d) % n
        for_owner(dest, lambda: to_owner(dest, me).wait_send())

    def drain():
        for d in range(1, n):
            to_reader((me + d) % n, me).wait_send()

    for_owner(me, drain)


def combine_kernel(am, sel, gate, own, out):
    back = jnp.dot(sel[:, 0 : own.shape[0]], own[...], preferred_element_type=F32)
    out[...] = (am[...].astype(F32) + gate[:, 0:1] * back).astype(BF16)


def solution(mesh):
    n = mesh.shape["seq"]

    def body(
        hid, gain, proj, bias, rate, mgain, fgain, router, routes, wg, wu, wd
    ):
        tok, width = hid.shape
        heads = bias.shape[0]
        lanes = width // heads
        cols = proj.shape[1]
        state = (cols - heads) // 2
        owners = min(n, heads)
        per = heads // owners
        chips = n // 2
        half_ring = chips // 2
        vm = pl.BlockSpec(memory_space=pltpu.VMEM)
        anyspec = pl.BlockSpec(memory_space=pl.ANY)
        dma = pltpu.SemaphoreType.DMA
        am, own, sel, gate = pl.pallas_call(
            functools.partial(block_kernel, n),
            out_shape=[
                jax.ShapeDtypeStruct((tok, width), BF16),
                jax.ShapeDtypeStruct((2 * CAP, width), BF16),
                jax.ShapeDtypeStruct((tok, 128), BF16),
                jax.ShapeDtypeStruct((tok, 128), F32),
            ],
            in_specs=[vm] * 9 + [anyspec] * 3,
            out_specs=[anyspec, vm, vm, vm],
            scratch_shapes=[
                pltpu.VMEM(wg.shape, BF16),
                pltpu.VMEM(wu.shape, BF16),
                pltpu.VMEM(wd.shape, BF16),
                pltpu.VMEM((tok, width), BF16),
                pltpu.VMEM((tok, width), F32),
                pltpu.VMEM((tok, width), BF16),
                pltpu.VMEM((tok, 128), F32),
                pltpu.VMEM((tok, 128), BF16),
                pltpu.VMEM((heads, tok), F32),
                pltpu.VMEM((heads, tok), F32),
                pltpu.VMEM((heads, tok), F32),
                pltpu.VMEM((state, tok), F32),
                pltpu.VMEM((tok, tok), F32),
                pltpu.VMEM((tok, cols), BF16),
                pltpu.VMEM((tok, cols), BF16),
                pltpu.VMEM((owners, state + 16, per * lanes), BF16),
                pltpu.VMEM((n, state + 16, per * lanes), BF16),
                pltpu.VMEM((n, state, per * lanes), BF16),
                pltpu.VMEM((owners, state, per * lanes), BF16),
                pltpu.VMEM((n, CAP, width), BF16),
                pltpu.VMEM((n, CAP, width), BF16),
                pltpu.VMEM((chips, CAP, width), BF16),
                pltpu.VMEM((2, half_ring, 2, CAP, width // 2), BF16),
                dma((3,)),
                dma,
                dma((n,)),
                dma((n,)),
                dma((n,)),
                dma((n,)),
                dma((2, half_ring, 2)),
                dma((2, half_ring, 2)),
                dma((2, half_ring + 1, 2)),
                dma((2, half_ring + 1, 2)),
                dma,
                dma,
                dma((2, half_ring, 2)),
                dma((2, half_ring, 2)),
            ],
            compiler_params=pltpu.CompilerParams(
                collective_id=0,
                has_side_effects=True,
                vmem_limit_bytes=60 * 1024 * 1024,
            ),
        )(
            hid,
            gain.reshape(1, width),
            proj,
            bias.reshape(heads, 1),
            rate.reshape(heads, 1),
            mgain.reshape(1, width),
            fgain.reshape(1, width),
            router,
            routes,
            wg,
            wu,
            wd,
        )
        block = width // 4
        return pl.pallas_call(
            combine_kernel,
            grid=(4,),
            out_shape=jax.ShapeDtypeStruct((tok, width), BF16),
            in_specs=[
                pl.BlockSpec((tok, block), lambda i: (0, i)),
                pl.BlockSpec((tok, 128), lambda i: (0, 0)),
                pl.BlockSpec((tok, 128), lambda i: (0, 0)),
                pl.BlockSpec((2 * CAP, block), lambda i: (0, i)),
            ],
            out_specs=pl.BlockSpec((tok, block), lambda i: (0, i)),
        )(am, sel, gate, own)

    both = P(("docs", "seq"), None)
    in_specs = (
        both, P(), P(), P(), P(), P(), P(), P(), both,
        P(None, "seq"), P(None, "seq"), P("seq", None),
    )
    return jax.shard_map(
        body, mesh=mesh, in_specs=in_specs, out_specs=both, check_vma=False
    )
```

time: 234 us -> 97.4 us (0.42)
  Pallas kernels: 0 us -> 81.7 us
  waiting for transfers between devices: 78.9 us -> 0 us
  blocking collectives: 74 us -> 0 us
  matrix products: 34.9 us -> 0 us
  between operations: 13.6 us -> 0.01 us
  other arithmetic: 11.6 us -> 0 us
  local copies, waits for them, and re-layouts: 19.6 us -> 15.3 us
    pallas_call x0 -> x2, Pallas kernels: none -> 81.7 us  [the longest x1 77.4 us: body(): pl.pallas_call(functools.partial(block_kernel, n), out_shape=[jax.ShapeDt...]
    all_gather x2 -> x0, waiting for transfers between devices: 78.8 us -> none  [the longest x1 56.7 us: body(): gathered = lax.all_gather(slot_rows, 'seq', axis=0, tiled=True)]
    all_to_all x1 -> x0, blocking collectives: 50.8 us -> none  [body(): lax.all_to_all(partial_value.astype(jnp.bfloat16), 'seq', split_axis=0, c...]
    dot_general x17 -> x0, matrix products: 34.9 us -> none  [the longest x1 6.56 us: body(): jnp.einsum('tn,hpn->thp', c_out, chain_in, precision=HIGHEST_MODE)]
    all_gather x1 -> x0, blocking collectives: 23.2 us -> none  [entering_2(): gathered = jax.tree.map(lambda a: lax.all_gather(a, axis), part)]
    unnamed x24 -> x7, local copies, waits for them, and re-layouts: 2.73 us -> 12.5 us
    reduce_sum x4 -> x0, other arithmetic: 6.28 us -> none  [the longest x2 5.96 us: rms_scale(): jnp.mean(values * values, axis=-1, keepdims=True) + EPSILON]
    mul x1 -> x0, local copies, waits for them, and re-layouts: 5.59 us -> none  [body(): ssm_out * lax.rsqrt(jnp.mean(ssm_out * ssm_out, axis=-1, keepdims=True) +...]
  transfers between devices with their start and end apart: 2 -> 0, of which waited for: 2 -> 0; matrix products, arithmetic and copies ran while one was open for 3% -> 0% of each run, Pallas kernels for 0% -> 0%
where the time goes in v1:
time: 97.4 us; the launch traced here: 97 us
  Pallas kernels  81.7 us (84%)
  local copies, waits for them, and re-layouts  15.3 us (16%)
    pallas_call x1, Pallas kernels, body(): pl.pallas_call(functools.partial(block_kernel, n), out_shape=[jax.ShapeDt...  77.4 us
    unnamed x7, local copies, waits for them, and re-layouts  12.5 us
    pallas_call x1, Pallas kernels, body(): pl.pallas_call(combine_kernel, grid=(4,), out_shape=jax.ShapeDtypeStruct(...  4.32 us

profile of v1, /device:TPU:0, one launch (start us, length us, event | category | flops | bytes accessed | tf_op | source)
XLA Modules:
  0.0 97.0 jit_solution(14376531323915539761)
XLA Ops:
  0.0 0.0 copy-start
  0.0 1.5 %copy.14.bias = f32[32,1]{1,0:T(8,128)} copy(f32[32,1]{0,1:T(1,128)} %bitcast.8) | data formatting | bytes 256 | tf_op jit(solution)/shard_map/reshape | solution.py:557
  1.5 1.3 %copy.15.rate = f32[32,1]{1,0:T(8,128)} copy(f32[32,1]{0,1:T(1,128)} %bitcast.9) | data formatting | bytes 256 | tf_op jit(solution)/shard_map/reshape | solution.py:558
  2.8 1.5 %copy.17.routes = s32[256,2]{1,0:T(8,128)} copy(s32[256,2]{0,1:T(2,128)} %param.20) | data formatting | bytes 4096 | tf_op args[8]
  4.3 2.3 %copy.13.proj = bf16[4096,64]{1,0:T(8,128)(2,1)} copy(bf16[4096,64]{0,1:T(8,128)(2,1)} %param.14) | data formatting | bytes 1048576 | tf_op args[2]
  6.6 2.3 %copy.16.router = bf16[4096,16]{1,0:T(8,128)(2,1)} copy(bf16[4096,16]{0,1:T(8,128)(2,1)} %param.19) | data formatting | bytes 262144 | tf_op args[7]
  8.9 0.0 copy-done
  8.9 2.4 %copy.18.wg_hbm = bf16[4096,224]{1,0:T(8,128)(2,1)} copy(bf16[4096,224]{0,1:T(8,128)(2,1)S(1)} %copy-done) | data formatting | bytes 3670016 | tf_op args[9]
  11.3 4.0 %copy.19.wu_hbm = bf16[4096,224]{1,0:T(8,128)(2,1)} copy(bf16[4096,224]{0,1:T(8,128)(2,1)} %param.22) | data formatting | bytes 3670016 | tf_op args[10]
  15.3 77.4 %shard_map.118 = (bf16[256,4096]{1,0:T(8,128)(2,1)}, bf16[32,4096]{1,0:T(8,128)(2,1)}, bf16[256,128]{1,0:T(8,128)(2,1)}, f32[256,128]{1,0:T(8,128)}) custom-call(bf16[256,4096]{1,0:T(8,128)(2,1)} %hid.1, f32[1,4096]{1,0:T(1,128)} %bitcast.5, bf16[4096,64]{1,0:T(8,128)(2,1)} %copy.13.proj, f32[32,1]{1,0:T(8,128)} %copy.14.bias, f32[32,1]{1,0:T(8,128)} %copy.15.rate, ...), custom_call_target="tpu_custom_call" | custom-call | tf_op jit(solution)/shard_map/pallas_call | solution.py:499
  92.7 4.3 %shard_map.119 = bf16[256,4096]{1,0:T(8,128)(2,1)} custom-call(bf16[256,4096]{1,0:T(8,128)(2,1)} %get-tuple-element.9.am, bf16[256,128]{1,0:T(8,128)(2,1)} %get-tuple-element.10.sel, f32[256,128]{1,0:T(8,128)} %get-tuple-element.11.gate, bf16[32,4096]{1,0:T(8,128)(2,1)} %get-tuple-element.12.own), custom_call_target="tpu_custom_call" | custom-call | tf_op jit(solution)/shard_map/pallas_call | solution.py:568
Async XLA Ops:
  0.0 8.9 %copy-start = (bf16[4096,224]{0,1:T(8,128)(2,1)S(1)}, bf16[4096,224]{0,1:T(8,128)(2,1)}, u32[]{:S(2)}) copy-start(bf16[4096,224]{0,1:T(8,128)(2,1)} %param.21) | copy-start | bytes 5505028

commit v2 on v1

--- a/solution.py
+++ b/solution.py
@@ -24,6 +24,10 @@
         device_id={"seq": target},
         device_id_type=MESH,
     )
+
+
+def across_last(a, b):
+    return lax.dot_general(a, b, (((1,), (1,)), ((), ())), preferred_element_type=F32)
 
 
 def iota(shape, dim):
@@ -47,14 +51,15 @@
     am_out,
     own_out,
     sel_out,
-    gate_out,
     wg,
     wu,
     wd,
     xn,
     within,
     am,
-    acc,
+    wsel,
+    hsel,
+    ysel,
     cum3,
     cumt,
     dtt,
@@ -87,9 +92,9 @@
     r_recv,
 ):
     tok, width = hid.shape
-    heads = bias.shape[0]
+    heads = bias.shape[1]
     lanes = width // heads
-    state = (proj.shape[1] - heads) // 2
+    state = (proj.shape[0] - heads) // 2
     owners = msg.shape[0]
     per = heads // owners
     chips = n // 2
@@ -134,16 +139,19 @@
 
     lax.fori_loop(0, tok // 16, norm_rows, 0)
 
-    p = jnp.dot(xn[...], proj[...], preferred_element_type=F32)
+    p = across_last(xn[...], proj[...])
     p_hi = p.astype(BF16)
     phi[...] = p_hi
     plo[...] = (p - p_hi.astype(F32)).astype(BF16)
     pt = p.T
     b_t = pt[0:state]
-    v = pt[2 * state :] + bias[...]
+    eye = iota((heads, heads), 0) == iota((heads, heads), 1)
+    bias_col = jnp.sum(jnp.where(eye, bias[...], 0.0), axis=1, keepdims=True)
+    rate_col = jnp.sum(jnp.where(eye, rate[...], 0.0), axis=1, keepdims=True)
+    v = pt[2 * state :] + bias_col
     dt = jnp.maximum(v, 0.0) + jnp.log(1.0 + jnp.exp(-jnp.abs(v)))
     upper = (iota((tok, tok), 0) <= iota((tok, tok), 1)).astype(F32)
-    c_t = jnp.dot(-dt * rate[...], upper, precision=HI, preferred_element_type=F32)
+    c_t = jnp.dot(-dt * rate_col, upper, precision=HI, preferred_element_type=F32)
     bt[...] = b_t
     dtt[...] = dt
     cumt[...] = c_t
@@ -214,6 +222,28 @@
     cross = jnp.dot(p, z, precision=HI, preferred_element_type=F32)
     crossm[...] = jnp.where(iota((tok, tok), 0) >= iota((tok, tok), 1), cross, 0.0)
 
+    r0 = routes[0:1, :]
+    r1 = routes[1:2, :]
+    hit = jnp.where((r0 == 0) | (r1 == 0), 1.0, 0.0)
+    other = jnp.where(r0 == 0, r1, r0).astype(F32)
+    wide = jnp.broadcast_to(hit, (CAP, tok))
+    rank = jnp.dot(
+        wide.astype(BF16), upper.astype(BF16), preferred_element_type=F32
+    )
+    sel_f = jnp.where((rank - 1.0).astype(jnp.int32) == iota((CAP, tok), 0), wide, 0.0)
+    other_sel = jnp.sum(sel_f * other, axis=1, keepdims=True)
+    sel = sel_f.astype(BF16)
+    blank = jnp.zeros((128 - 2 * CAP, tok), F32)
+    sel_out[...] = jnp.concatenate([sel_f, sel_f, blank], axis=0).T.astype(BF16)
+
+    def pick(value):
+        return jnp.dot(sel, value, preferred_element_type=F32).astype(BF16)
+
+    hsel[...] = pick(hid[...])
+    phi_sel = pick(phi[...])
+    plo_sel = pick(plo[...])
+    cum_sel = pick(cum3[...])
+
     mid = tok // 2
 
     def within_head(h, _):
@@ -221,6 +251,7 @@
         ch = jnp.dot(cum3[...], spread(h), preferred_element_type=F32)
         crow = cumt[pl.ds(h, 1), :]
         drow = dtt[pl.ds(h, 1), :]
+        chosen = None
         for k in range(2):
             rows = slice(k * mid, (k + 1) * mid)
             total = None
@@ -233,6 +264,13 @@
                 )
                 total = term if total is None else total + term
             within[rows, cols] = total
+            top = total.astype(BF16)
+            low = (total - top.astype(F32)).astype(BF16)
+            got = jnp.dot(
+                sel[:, rows], top, preferred_element_type=F32
+            ) + jnp.dot(sel[:, rows], low, preferred_element_type=F32)
+            chosen = got if chosen is None else chosen + got
+        wsel[:, cols] = chosen
         return 0
 
     lax.fori_loop(0, heads // 2, within_head, 0)
@@ -262,57 +300,41 @@
         source = (me + d) % n
         for_owner(source, lambda: to_reader(0, source).wait_recv())
 
-    acc[...] = jnp.zeros_like(acc)
-
-    def mix_head(h, _):
+    def mixed(h, c_hi, c_lo, cum, inside, base):
         cols = pl.ds(pl.multiple_of(h * lanes, lanes), lanes)
         inner = pl.ds(pl.multiple_of((h % per) * lanes, lanes), lanes)
         e = ent[h // per, :, inner]
         zero = jnp.zeros((state, lanes), BF16)
         rest = jnp.zeros((phi.shape[1] - 2 * state, lanes), BF16)
         ez = jnp.concatenate([zero, e, rest], axis=0)
-        carried = jnp.dot(phi[...], ez, preferred_element_type=F32) + jnp.dot(
-            plo[...], ez, preferred_element_type=F32
-        )
-        ch = jnp.dot(cum3[...], spread(h), preferred_element_type=F32)
-        o = within[:, cols] + jnp.exp(ch) * carried
+        carried = jnp.dot(c_hi, ez, preferred_element_type=F32) + jnp.dot(
+            c_lo, ez, preferred_element_type=F32
+        )
+        ch = jnp.dot(cum, spread(h), preferred_element_type=F32)
+        o = inside[:, cols] + jnp.exp(ch) * carried
         ms = jnp.mean(o * o, axis=-1, keepdims=True)
-        y = hid[:, cols].astype(F32) + o * lax.rsqrt(ms + EPS) * mgain[:, cols]
-        y = y.astype(BF16)
-        am[:, cols] = y
-        yf = y.astype(F32)
-        acc[...] += yf * yf
+        y = base[:, cols].astype(F32) + o * lax.rsqrt(ms + EPS) * mgain[:, cols]
+        return y.astype(BF16)
+
+    def mix_chosen(i, _):
+        for k in range(4):
+            h = i * 4 + k
+            cols = pl.ds(pl.multiple_of(h * lanes, lanes), lanes)
+            ysel[:, cols] = mixed(h, phi_sel, plo_sel, cum_sel, wsel, hsel)
         return 0
 
-    lax.fori_loop(0, heads, mix_head, 0)
-
-    am_copy = pltpu.make_async_copy(am, am_out, am_sem)
-    am_copy.start()
-
-    total = jnp.sum(acc[...], axis=-1, keepdims=True)
-    acc[...] = jnp.broadcast_to(lax.rsqrt(total / width + EPS), acc.shape)
-
-    def ffn_rows(i, _):
-        rows = pl.ds(pl.multiple_of(i * 16, 16), 16)
-        x = am[rows, :].astype(F32)
-        xn[rows, :] = (x * acc[rows, 0:1] * fgain[...]).astype(BF16)
+    lax.fori_loop(0, heads // 4, mix_chosen, 0)
+
+    x = ysel[...].astype(F32)
+    ms = jnp.mean(x * x, axis=-1, keepdims=True)
+    chosen_in = (x * lax.rsqrt(ms + EPS) * fgain[...]).astype(BF16)
+    mine = slot_at(pos, core)
+    gath[mine] = chosen_in
+
+    def mix_head(h, _):
+        cols = pl.ds(pl.multiple_of(h * lanes, lanes), lanes)
+        am[:, cols] = mixed(h, phi[...], plo[...], cum3[...], within, hid)
         return 0
-
-    lax.fori_loop(0, tok // 16, ffn_rows, 0)
-
-    r0 = routes[:, 0:1]
-    r1 = routes[:, 1:2]
-    hit = jnp.where((r0 == 0) | (r1 == 0), 1.0, 0.0)
-    lower = (iota((tok, tok), 0) >= iota((tok, tok), 1)).astype(BF16)
-    wide = jnp.broadcast_to(hit, (tok, 128))
-    rank = jnp.dot(lower, wide.astype(BF16), preferred_element_type=F32)
-    lane = iota((tok, 128), 1)
-    place = (rank - 1.0).astype(jnp.int32)
-    sel_t = jnp.where(((lane % CAP) == place) & (lane < 2 * CAP), wide, 0.0)
-    sel = sel_t.T[0:CAP].astype(BF16)
-    sel_out[...] = sel_t.astype(BF16)
-    mine = slot_at(pos, core)
-    gath[mine] = jnp.dot(sel, xn[...], preferred_element_type=F32).astype(BF16)
 
     def cut(h):
         return pl.ds(h * hw, hw)
@@ -361,13 +383,16 @@
     for h in range(2):
         go(own_across(h, mine))
 
-    logits = jnp.dot(xn[...], router[...], preferred_element_type=F32)
-    other = jnp.where(r0 == 0, r1, r0)
+    logits = across_last(chosen_in, router[...])
     picked = jnp.sum(
-        jnp.where(iota(logits.shape, 1) == other, logits, 0.0), axis=1, keepdims=True
+        jnp.where(iota(logits.shape, 1) == other_sel.astype(jnp.int32), logits, 0.0),
+        axis=1,
+        keepdims=True,
     )
-    gate = jnp.where(hit > 0.0, 1.0 / (1.0 + jnp.exp(picked - logits[:, 0:1])), 0.0)
-    gate_out[...] = jnp.broadcast_to(gate, gate_out.shape)
+    gate = 1.0 / (1.0 + jnp.exp(picked - logits[:, 0:1]))
+
+    pieces = 2 * half_ring
+    done = 0
 
     for s in range(half_ring):
         for h in range(2):
@@ -381,6 +406,11 @@
                 if s + 1 < half_ring and used(way, s + 1, hh):
                     go(ring(way, s + 1, hh, place))
                 go(across(way, s, hh, place, core))
+            upto = (2 * s + h + 1) * heads // pieces
+            lax.fori_loop(done, upto, mix_head, 0)
+            done = upto
+    am_copy = pltpu.make_async_copy(am, am_out, am_sem)
+    am_copy.start()
     for h in range(2):
         own_across(h, slot_at(pos, 1 - core)).wait_recv()
     for s in range(half_ring):
@@ -394,29 +424,42 @@
         load.wait()
     rows_all = n * CAP
     x_all = gath[...].reshape(rows_all, width)
-    g = jnp.dot(x_all, wg[...], preferred_element_type=F32)
-    u = jnp.dot(x_all, wu[...], preferred_element_type=F32)
+    g = across_last(x_all, wg[...])
+    u = across_last(x_all, wu[...])
     hidden = (g / (1.0 + jnp.exp(-g)) * u).astype(BF16)
-    step_w = 512
-    for k in range(width // step_w):
-        c = slice(k * step_w, (k + 1) * step_w)
-        part[:, :, c] = (
-            jnp.dot(hidden, wd[:, c], preferred_element_type=F32)
-            .astype(BF16)
-            .reshape(n, CAP, step_w)
-        )
-    swap = remote(
-        part.at[pl.ds((1 - core) * chips, chips)], prt, p_send, p_recv, partner
-    )
-    go(swap)
-    swap.wait_recv()
-
-    def pair_sum(i, _):
-        at = core * chips + i
-        part[at] = (part[at].astype(F32) + prt[i].astype(F32)).astype(BF16)
-        return 0
-
-    lax.fori_loop(0, chips, pair_sum, 0)
+    step_w = hw // 4
+
+    def swap(h):
+        return remote(
+            part.at[pl.ds((1 - core) * chips, chips), :, cut(h)],
+            prt.at[:, :, cut(h)],
+            p_send.at[h],
+            p_recv.at[h],
+            partner,
+        )
+
+    for h in range(2):
+        for k in range(4):
+            c = slice(h * hw + k * step_w, h * hw + (k + 1) * step_w)
+            part[:, :, c] = (
+                jnp.dot(hidden, wd[:, c], preferred_element_type=F32)
+                .astype(BF16)
+                .reshape(n, CAP, step_w)
+            )
+        go(swap(h))
+
+    def pair_sum(h):
+        swap(h).wait_recv()
+        cc = slice(h * hw, (h + 1) * hw)
+
+        def one(i, _):
+            at = core * chips + i
+            part[at, :, cc] = (
+                part[at, :, cc].astype(F32) + prt[i, :, cc].astype(F32)
+            ).astype(BF16)
+            return 0
+
+        lax.fori_loop(0, chips, one, 0)
 
     def reduce_copy(way, s, h):
         step = 1 - 2 * way
@@ -438,6 +481,8 @@
                 hh = h if way == 0 else 1 - h
                 if not carries(way, s, hh):
                     continue
+                if s == 0:
+                    pair_sum(hh)
                 if s > 0 and carries(way, s - 1, hh):
                     reduce_copy(way, s - 1, hh).wait_recv()
                     step = 1 - 2 * way
@@ -455,6 +500,7 @@
             if carries(way, half_ring - 1, h):
                 reduce_copy(way, half_ring - 1, h).wait_recv()
                 own += rbuf[way, half_ring - 1, h].astype(F32)
+        own = own * gate
         own_hi = own.astype(BF16)
         own_out[0:CAP, cc] = own_hi
         own_out[CAP : 2 * CAP, cc] = (own - own_hi.astype(F32)).astype(BF16)
@@ -473,9 +519,9 @@
     for_owner(me, drain)
 
 
-def combine_kernel(am, sel, gate, own, out):
+def combine_kernel(am, sel, own, out):
     back = jnp.dot(sel[:, 0 : own.shape[0]], own[...], preferred_element_type=F32)
-    out[...] = (am[...].astype(F32) + gate[:, 0:1] * back).astype(BF16)
+    out[...] = (am[...].astype(F32) + back).astype(BF16)
 
 
 def solution(mesh):
@@ -496,24 +542,25 @@
         vm = pl.BlockSpec(memory_space=pltpu.VMEM)
         anyspec = pl.BlockSpec(memory_space=pl.ANY)
         dma = pltpu.SemaphoreType.DMA
-        am, own, sel, gate = pl.pallas_call(
+        am, own, sel = pl.pallas_call(
             functools.partial(block_kernel, n),
             out_shape=[
                 jax.ShapeDtypeStruct((tok, width), BF16),
                 jax.ShapeDtypeStruct((2 * CAP, width), BF16),
                 jax.ShapeDtypeStruct((tok, 128), BF16),
-                jax.ShapeDtypeStruct((tok, 128), F32),
             ],
             in_specs=[vm] * 9 + [anyspec] * 3,
-            out_specs=[anyspec, vm, vm, vm],
+            out_specs=[anyspec, vm, vm],
             scratch_shapes=[
-                pltpu.VMEM(wg.shape, BF16),
-                pltpu.VMEM(wu.shape, BF16),
+                pltpu.VMEM(wg.shape[::-1], BF16),
+                pltpu.VMEM(wu.shape[::-1], BF16),
                 pltpu.VMEM(wd.shape, BF16),
                 pltpu.VMEM((tok, width), BF16),
                 pltpu.VMEM((tok, width), F32),
                 pltpu.VMEM((tok, width), BF16),
-                pltpu.VMEM((tok, 128), F32),
+                pltpu.VMEM((CAP, width), F32),
+                pltpu.VMEM((CAP, width), BF16),
+                pltpu.VMEM((CAP, width), BF16),
                 pltpu.VMEM((tok, 128), BF16),
                 pltpu.VMEM((heads, tok), F32),
                 pltpu.VMEM((heads, tok), F32),
@@ -540,8 +587,8 @@
                 dma((2, half_ring, 2)),
                 dma((2, half_ring + 1, 2)),
                 dma((2, half_ring + 1, 2)),
-                dma,
-                dma,
+                dma((2,)),
+                dma((2,)),
                 dma((2, half_ring, 2)),
                 dma((2, half_ring, 2)),
             ],
@@ -553,15 +600,15 @@
         )(
             hid,
             gain.reshape(1, width),
-            proj,
-            bias.reshape(heads, 1),
-            rate.reshape(heads, 1),
+            proj.T,
+            bias.reshape(1, heads),
+            rate.reshape(1, heads),
             mgain.reshape(1, width),
             fgain.reshape(1, width),
-            router,
-            routes,
-            wg,
-            wu,
+            router.T,
+            routes.T,
+            wg.T,
+            wu.T,
             wd,
         )
         block = width // 4
@@ -572,11 +619,10 @@
             in_specs=[
                 pl.BlockSpec((tok, block), lambda i: (0, i)),
                 pl.BlockSpec((tok, 128), lambda i: (0, 0)),
-                pl.BlockSpec((tok, 128), lambda i: (0, 0)),
                 pl.BlockSpec((2 * CAP, block), lambda i: (0, i)),
             ],
             out_specs=pl.BlockSpec((tok, block), lambda i: (0, i)),
-        )(am, sel, gate, own)
+        )(am, sel, own)
 
     both = P(("docs", "seq"), None)
     in_specs = (

time: 97.4 us -> 73.9 us (0.76)
  local copies, waits for them, and re-layouts: 15.3 us -> 0 us
  Pallas kernels: 81.7 us -> 73.6 us
    unnamed x7 -> x0, local copies, waits for them, and re-layouts: 12.5 us -> none
    pallas_call x1, Pallas kernels: 77.4 us -> 69.4 us  [body(): pl.pallas_call(functools.partial(block_kernel, n), out_shape=[jax.ShapeDt...]
    reshape x2 -> x0, local copies, waits for them, and re-layouts: 2.81 us -> none  [the longest x1 1.48 us: body(): bias.reshape(heads, 1)]
where the time goes in v2:
time: 73.9 us; the launch traced here: 73.6 us
  Pallas kernels  73.6 us (100%)
    pallas_call x1, Pallas kernels, body(): pl.pallas_call(functools.partial(block_kernel, n), out_shape=[jax.ShapeDt...  69.4 us
    pallas_call x1, Pallas kernels, body(): pl.pallas_call(combine_kernel, grid=(4,), out_shape=jax.ShapeDtypeStruct(...  4.27 us

profile of v2, /device:TPU:0, one launch (start us, length us, event | category | flops | bytes accessed | tf_op | source)
XLA Modules:
  0.0 73.6 jit_solution(15275030061948464283)
XLA Ops:
  0.0 69.4 %shard_map.118 = (bf16[256,4096]{1,0:T(8,128)(2,1)}, bf16[32,4096]{1,0:T(8,128)(2,1)}, bf16[256,128]{1,0:T(8,128)(2,1)}) custom-call(bf16[256,4096]{1,0:T(8,128)(2,1)} %hid.1, f32[1,4096]{1,0:T(1,128)} %bitcast.14, bf16[64,4096]{1,0:T(8,128)(2,1)} %bitcast.12, f32[1,32]{1,0:T(1,128)} %bitcast.18, f32[1,32]{1,0:T(1,128)} %bitcast.19, f32[1,4096]{1,0:T(1,128)} %bitcast.15, ...), custom_call_target="tpu_custom_call" | custom-call | tf_op jit(solution)/shard_map/pallas_call | solution.py:545
  69.4 4.3 %shard_map.119 = bf16[256,4096]{1,0:T(8,128)(2,1)} custom-call(bf16[256,4096]{1,0:T(8,128)(2,1)} %get-tuple-element.8.am, bf16[256,128]{1,0:T(8,128)(2,1)} %get-tuple-element.9.sel, bf16[32,4096]{1,0:T(8,128)(2,1)} %get-tuple-element.10.own), custom_call_target="tpu_custom_call" | custom-call | tf_op jit(solution)/shard_map/pallas_call | solution.py:615

commit v3 on v2

--- a/solution.py
+++ b/solution.py
@@ -8,6 +8,7 @@
 from jax.sharding import PartitionSpec as P
 
 CAP = 16
+CUTS = 4
 EPS = 1e-05
 HI = lax.Precision.HIGHEST
 MESH = pl.DeviceIdType.MESH
@@ -99,7 +100,8 @@
     per = heads // owners
     chips = n // 2
     half_ring = chips // 2
-    hw = width // 2
+    hw = width // CUTS
+    near = CUTS // 2
     me = lax.axis_index("seq")
     core = me % 2
     chip = me // 2
@@ -363,11 +365,11 @@
         started.append(copy)
 
     def used(way, s, h):
-        return s < half_ring - 1 or h == way
-
-    for h in range(2):
+        return s < half_ring - 1 or h // near == way
+
+    for h in range(CUTS):
         for way in range(2):
-            hh = h if way == 0 else 1 - h
+            hh = (h + near * way) % CUTS
             if used(way, 0, hh):
                 go(ring(way, 0, hh, pos))
     def own_across(h, slot):
@@ -375,12 +377,12 @@
         return remote(
             block,
             block,
-            d_send.at[h, half_ring, 0],
-            d_recv.at[h, half_ring, 0],
+            d_send.at[0, half_ring, h],
+            d_recv.at[0, half_ring, h],
             partner,
         )
 
-    for h in range(2):
+    for h in range(CUTS):
         go(own_across(h, mine))
 
     logits = across_last(chosen_in, router[...])
@@ -391,13 +393,13 @@
     )
     gate = 1.0 / (1.0 + jnp.exp(picked - logits[:, 0:1]))
 
-    pieces = 2 * half_ring
+    pieces = CUTS * half_ring
     done = 0
 
     for s in range(half_ring):
-        for h in range(2):
+        for h in range(CUTS):
             for way in range(2):
-                hh = h if way == 0 else 1 - h
+                hh = (h + near * way) % CUTS
                 if not used(way, s, hh):
                     continue
                 step = 1 - 2 * way
@@ -406,16 +408,16 @@
                 if s + 1 < half_ring and used(way, s + 1, hh):
                     go(ring(way, s + 1, hh, place))
                 go(across(way, s, hh, place, core))
-            upto = (2 * s + h + 1) * heads // pieces
+            upto = (CUTS * s + h + 1) * heads // pieces
             lax.fori_loop(done, upto, mix_head, 0)
             done = upto
     am_copy = pltpu.make_async_copy(am, am_out, am_sem)
     am_copy.start()
-    for h in range(2):
+    for h in range(CUTS):
         own_across(h, slot_at(pos, 1 - core)).wait_recv()
     for s in range(half_ring):
         for way in range(2):
-            for h in range(2):
+            for h in range(CUTS):
                 if used(way, s, h):
                     step = 1 - 2 * way
                     across(way, s, h, pos - step * (1 + s), 1 - core).wait_recv()
@@ -427,7 +429,6 @@
     g = across_last(x_all, wg[...])
     u = across_last(x_all, wu[...])
     hidden = (g / (1.0 + jnp.exp(-g)) * u).astype(BF16)
-    step_w = hw // 4
 
     def swap(h):
         return remote(
@@ -438,14 +439,14 @@
             partner,
         )
 
-    for h in range(2):
-        for k in range(4):
-            c = slice(h * hw + k * step_w, h * hw + (k + 1) * step_w)
-            part[:, :, c] = (
-                jnp.dot(hidden, wd[:, c], preferred_element_type=F32)
-                .astype(BF16)
-                .reshape(n, CAP, step_w)
-            )
+    for k in range(CUTS):
+        h = (k // 2) + near * (k % 2)
+        c = slice(h * hw, (h + 1) * hw)
+        part[:, :, c] = (
+            jnp.dot(hidden, wd[:, c], preferred_element_type=F32)
+            .astype(BF16)
+            .reshape(n, CAP, hw)
+        )
         go(swap(h))
 
     def pair_sum(h):
@@ -473,12 +474,12 @@
         )
 
     def carries(way, s, h):
-        return s > 0 or h == way
+        return s > 0 or h // near == way
 
     for s in range(half_ring):
-        for h in range(2):
+        for h in range(CUTS):
             for way in range(2):
-                hh = h if way == 0 else 1 - h
+                hh = (h + near * way) % CUTS
                 if not carries(way, s, hh):
                     continue
                 if s == 0:
@@ -493,7 +494,7 @@
                         + rbuf[way, s - 1, hh].astype(F32)
                     ).astype(BF16)
                 go(reduce_copy(way, s, hh))
-    for h in range(2):
+    for h in range(CUTS):
         cc = slice(h * hw, (h + 1) * hw)
         own = part[mine, :, cc].astype(F32)
         for way in range(2):
@@ -576,21 +577,21 @@
                 pltpu.VMEM((n, CAP, width), BF16),
                 pltpu.VMEM((n, CAP, width), BF16),
                 pltpu.VMEM((chips, CAP, width), BF16),
-                pltpu.VMEM((2, half_ring, 2, CAP, width // 2), BF16),
+                pltpu.VMEM((2, half_ring, CUTS, CAP, width // CUTS), BF16),
                 dma((3,)),
                 dma,
                 dma((n,)),
                 dma((n,)),
                 dma((n,)),
                 dma((n,)),
-                dma((2, half_ring, 2)),
-                dma((2, half_ring, 2)),
-                dma((2, half_ring + 1, 2)),
-                dma((2, half_ring + 1, 2)),
-                dma((2,)),
-                dma((2,)),
-                dma((2, half_ring, 2)),
-                dma((2, half_ring, 2)),
+                dma((2, half_ring, CUTS)),
+                dma((2, half_ring, CUTS)),
+                dma((2, half_ring + 1, CUTS)),
+                dma((2, half_ring + 1, CUTS)),
+                dma((CUTS,)),
+                dma((CUTS,)),
+                dma((2, half_ring, CUTS)),
+                dma((2, half_ring, CUTS)),
             ],
             compiler_params=pltpu.CompilerParams(
                 collective_id=0,
@@ -611,10 +612,10 @@
             wu.T,
             wd,
         )
-        block = width // 4
+        block = width // 8
         return pl.pallas_call(
             combine_kernel,
-            grid=(4,),
+            grid=(8,),
             out_shape=jax.ShapeDtypeStruct((tok, width), BF16),
             in_specs=[
                 pl.BlockSpec((tok, block), lambda i: (0, i)),

time: 73.9 us -> 73.4 us (level)
    pallas_call x1, Pallas kernels: 69.4 us -> 66.8 us  [body(): pl.pallas_call(functools.partial(block_kernel, n), out_shape=[jax.ShapeDt...]
    pallas_call x1, Pallas kernels: 4.27 us -> 6.32 us  [body(): pl.pallas_call(combine_kernel, grid=(8,), out_shape=jax.ShapeDtypeStruct(...]
where the time goes in v3:
time: 73.4 us; the launch traced here: 73.1 us
  Pallas kernels  73.1 us (100%)
    pallas_call x1, Pallas kernels, body(): pl.pallas_call(functools.partial(block_kernel, n), out_shape=[jax.ShapeDt...  66.8 us
    pallas_call x1, Pallas kernels, body(): pl.pallas_call(combine_kernel, grid=(8,), out_shape=jax.ShapeDtypeStruct(...  6.32 us

profile of v3, /device:TPU:0, one launch (start us, length us, event | category | flops | bytes accessed | tf_op | source)
XLA Modules:
  0.0 73.1 jit_solution(10236204836735115511)
XLA Ops:
  0.0 66.8 %shard_map.118 = (bf16[256,4096]{1,0:T(8,128)(2,1)}, bf16[32,4096]{1,0:T(8,128)(2,1)}, bf16[256,128]{1,0:T(8,128)(2,1)}) custom-call(bf16[256,4096]{1,0:T(8,128)(2,1)} %hid.1, f32[1,4096]{1,0:T(1,128)} %bitcast.14, bf16[64,4096]{1,0:T(8,128)(2,1)} %bitcast.12, f32[1,32]{1,0:T(1,128)} %bitcast.18, f32[1,32]{1,0:T(1,128)} %bitcast.19, f32[1,4096]{1,0:T(1,128)} %bitcast.15, ...), custom_call_target="tpu_custom_call" | custom-call | tf_op jit(solution)/shard_map/pallas_call | solution.py:546
  66.8 6.3 %shard_map.119 = bf16[256,4096]{1,0:T(8,128)(2,1)} custom-call(bf16[256,4096]{1,0:T(8,128)(2,1)} %get-tuple-element.8.am, bf16[256,128]{1,0:T(8,128)(2,1)} %get-tuple-element.9.sel, bf16[32,4096]{1,0:T(8,128)(2,1)} %get-tuple-element.10.own), custom_call_target="tpu_custom_call" | custom-call | tf_op jit(solution)/shard_map/pallas_call | solution.py:616
